TPU v7x, 32 devices: a whole 2x2x4 slice. The times are simulated.
32 devices in a mesh: trans: 16 (over z, y, x), los: 2 (over core).
Axes of the slice: x: 2, y: 2, z: 4, core: 2. Of those that a mesh axis runs over, the one named last changes fastest.
Arguments:
- density: bfloat16 [2, 2048, 2048], P('los', 'trans'), may hold values from -6 to 6
- row_pos: float32 [2, 2048], replicated, may hold values from 0 to 2048
- col_pos: float32 [2, 2048], replicated, may hold values from 0 to 2048
- plane_of_slot: int32 [2], replicated, may hold values from 0 to 1, each once
- plane_bin: int32 [2], replicated, may hold values from 0 to 3, as said below
- efficiency: float32 [4, 2], replicated, may hold values from 0.3 to 3
Outputs:
- shear: float32 [2, 4, 2048, 2048], P(None, None, ('trans', 'los'))
Inputs may be any that keep to these rules, and one draw needn't show every extreme that they name: `plane_bin`: some plane has bin 0 and some plane has bin 4 - 1.
All inputs are finite; a program needn't handle non-finite values.
Results may differ from a plain program's by a relative error of at most 0.006.
Values may be sent and summed in bfloat16 or wider, within the bound.
A program may use at most 64 MiB of HBM per device.

v0:
```python
import math
import jax
import jax.numpy as jnp
from jax import lax
from jax.sharding import PartitionSpec as P


def hat_block(positions, mesh_cells):
    cells = jnp.arange(mesh_cells, dtype=jnp.int32).astype(jnp.float32)
    offset = positions[:, None] - cells[None, :] + 0.5 * mesh_cells
    folded = jnp.mod(offset, 1.0 * mesh_cells) - 0.5 * mesh_cells
    return jnp.maximum(1.0 - jnp.abs(folded), 0.0).astype(jnp.bfloat16)


def trig_pair(rows_n, cols_n, modulus, sign_value):
    product_index = (
        jnp.arange(rows_n, dtype=jnp.int32)[:, None]
        * jnp.arange(cols_n, dtype=jnp.int32)[None, :]
        % modulus
    )
    angle = product_index.astype(jnp.float32) * (2.0 * math.pi / modulus)
    return (jnp.cos(angle), sign_value * jnp.sin(angle))


def fourier(real_part, imag_part, inverse):
    length = real_part.shape[-1]
    factor_one = 16
    second = length // factor_one
    sign_value = 1.0 if inverse else -1.0
    lead_shape = real_part.shape[:-1]
    highest = lax.Precision.HIGHEST
    cos_one, sin_one = trig_pair(factor_one, factor_one, factor_one, sign_value)
    real_grid = real_part.reshape(lead_shape + (factor_one, second))
    imag_grid = imag_part.reshape(lead_shape + (factor_one, second))

    def first_pass(table, values):
        return jnp.einsum("kn,...nm->...km", table, values, precision=highest)

    section_real = first_pass(cos_one, real_grid) - first_pass(sin_one, imag_grid)
    section_imag = first_pass(cos_one, imag_grid) + first_pass(sin_one, real_grid)
    cos_twid, sin_twid = trig_pair(factor_one, second, length, sign_value)
    turned_real = section_real * cos_twid - section_imag * sin_twid
    turned_imag = section_real * sin_twid + section_imag * cos_twid
    cos_two, sin_two = trig_pair(second, second, second, sign_value)

    def second_pass(values, table):
        return jnp.einsum("...km,mj->...kj", values, table, precision=highest)

    out_real = second_pass(turned_real, cos_two) - second_pass(turned_imag, sin_two)
    out_imag = second_pass(turned_real, sin_two) + second_pass(turned_imag, cos_two)
    out_real = jnp.swapaxes(out_real, -1, -2).reshape(lead_shape + (length,))
    out_imag = jnp.swapaxes(out_imag, -1, -2).reshape(lead_shape + (length,))
    scale = 1.0 / length if inverse else 1.0
    return (out_real * scale, out_imag * scale)


def wave_numbers(index_all, length):
    return jnp.where(index_all < length // 2, index_all, index_all - length).astype(jnp.float32)


def body(density, row_pos, col_pos, plane_of_slot, plane_bin, efficiency):
    count_trans = lax.axis_size("trans")
    count_los = lax.axis_size("los")
    per_device = density.shape[0]
    mesh_cells = density.shape[2]
    grid_cells = row_pos.shape[1]
    planes_total = row_pos.shape[0]
    bins_total = efficiency.shape[0]
    width_cols = grid_cells // (count_trans * count_los)
    block_rows = min(512, grid_cells)
    slots = jnp.arange(planes_total, dtype=jnp.int32)
    bin_index = jnp.arange(bins_total, dtype=jnp.int32)
    by_columns = lax.all_to_all(density, "trans", split_axis=2, concat_axis=1, tiled=True)
    local_slot = 0
    slot_now = lax.axis_index("los") * per_device + local_slot
    plane_id = jnp.sum(jnp.where(slots == slot_now, plane_of_slot, 0))
    chosen = slots == plane_id
    plane_eff = jnp.sum(jnp.where(chosen[None, :], efficiency, 0.0), axis=1)
    first_bin = jnp.sum(jnp.where(chosen, plane_bin, 0))
    weight_list = [plane_eff * (bin_index >= first_bin).astype(jnp.float32)]
    rows_here = jnp.sum(jnp.where(chosen[:, None], row_pos, 0.0), axis=0)
    cols_here = jnp.sum(jnp.where(chosen[:, None], col_pos, 0.0), axis=0)
    pieces = []
    for begin in range(0, grid_cells, block_rows):
        row_block = hat_block(rows_here[begin : begin + block_rows], mesh_cells)
        pieces.append(
            lax.dot_general(
                by_columns[local_slot],
                row_block,
                (((0,), (1,)), ((), ())),
                preferred_element_type=jnp.float32,
            )
        )
    resampled = [jnp.concatenate(pieces, axis=1).astype(jnp.bfloat16)]
    col_tables = [hat_block(cols_here, mesh_cells)]
    half_columns = jnp.stack(resampled)
    exchanged = lax.all_to_all(half_columns, "trans", split_axis=2, concat_axis=1, tiled=True)
    local_slot = 0
    rows_map = lax.dot_general(
        exchanged[local_slot],
        col_tables[local_slot],
        (((0,), (1,)), ((), ())),
        preferred_element_type=jnp.float32,
    )
    plane_term = weight_list[local_slot][None, :, None] * rows_map[:, None, :]
    term_real, term_imag = fourier(plane_term, jnp.zeros_like(plane_term), False)
    summed_real, summed_imag = (
        lax.psum_scatter(term_real, "los", scatter_dimension=2, tiled=True),
        lax.psum_scatter(term_imag, "los", scatter_dimension=2, tiled=True),
    )
    arrived = lax.all_to_all(
        jnp.stack([summed_real, summed_imag]), "trans", split_axis=3, concat_axis=1, tiled=True
    )
    columns_local = arrived.transpose(0, 2, 3, 1)
    col_index = (
        lax.axis_index("los") * (grid_cells // count_los)
        + lax.axis_index("trans") * width_cols
        + jnp.arange(width_cols, dtype=jnp.int32)
    )
    freq_real, freq_imag = fourier(columns_local[0], columns_local[1], False)
    wave_rows = wave_numbers(jnp.arange(grid_cells, dtype=jnp.int32), grid_cells)[None, :]
    wave_cols = wave_numbers(col_index, grid_cells)[:, None]
    square_sum = jnp.maximum(wave_rows * wave_rows + wave_cols * wave_cols, 1.0)
    first_factor = (wave_rows * wave_rows - wave_cols * wave_cols) / square_sum
    second_factor = 2.0 * wave_rows * wave_cols / square_sum
    kernel_real = first_factor * freq_real - second_factor * freq_imag
    kernel_imag = first_factor * freq_imag + second_factor * freq_real
    back_real, back_imag = fourier(kernel_real, kernel_imag, True)
    returned = jnp.stack([back_real, back_imag]).transpose(0, 3, 1, 2)
    rows_local = lax.all_to_all(
        lax.all_to_all(returned, "trans", split_axis=1, concat_axis=3, tiled=True),
        "los",
        split_axis=1,
        concat_axis=3,
        tiled=True,
    )
    final_real, final_imag = fourier(rows_local[0], rows_local[1], True)
    return jnp.stack([final_real, final_imag]).transpose(0, 2, 1, 3)


def solution(mesh):
    placed = (P("los", "trans", None), P(), P(), P(), P(), P())
    return jax.shard_map(
        body,
        mesh=mesh,
        in_specs=placed,
        out_specs=P(None, None, ("trans", "los"), None),
        check_vma=False,
    )
```

profile of v0, /device:TPU:0, one launch (start us, length us, event | category | flops | bytes accessed | tf_op | source)
XLA Modules:
  0.0 628.0 jit_solution(389081637381458077)
XLA Ops:
  9.4 11.4 %reduce = bf16[2048,128]{1,0:T(8,128)(2,1)S(1)} reduce(bf16[2048,1,128]{2,1,0:T(2,128)(2,1)S(1)} %bitcast.333, bf16[]{:T(256)} %broadcast.788), dimensions={1}, to_apply=%bitcast.274.reduce_sub_computation | reduce | bytes 1048578
  21.8 8.9 %all-to-all-start = ((bf16[16,2,8192]{2,1,0:T(2,128)(2,1)}), bf16[16,2,8192]{2,1,0:T(2,128)(2,1)S(1)}, u32[]{:S(2)}, u32[]{:S(2)}) async-start(bf16[16,2,8192]{2,1,0:T(2,128)(2,1)} %reshape.416), calls=%async_computation | async-start | bytes 1048576 | tf_op jit(solution)/shard_map/all_to_all | solution.py:73
  32.2 13.6 %all-to-all-done = bf16[16,2,8192]{2,1,0:T(2,128)(2,1)S(1)} async-done(((bf16[16,2,8192]{2,1,0:T(2,128)(2,1)}), bf16[16,2,8192]{2,1,0:T(2,128)(2,1)S(1)}, u32[]{:S(2)}, u32[]{:S(2)}) %all-to-all-start) | async-done | bytes 524320 | tf_op jit(solution)/shard_map/all_to_all | solution.py:73
  61.7 8.1 %copy.182 = bf16[1,128,2048]{1,0,2:T(2,128)(2,1)S(1)} copy(bf16[1,128,2048]{1,2,0:T(8,128)(2,1)S(1)} %pad_maximum_fusion.1) | data formatting | bytes 1048576 | tf_op jit(solution)/shard_map/concatenate | solution.py:94
  69.9 11.6 %reduce.1 = bf16[2048,128]{1,0:T(8,128)(2,1)S(1)} reduce(bf16[2048,1,128]{2,1,0:T(2,128)(2,1)S(1)} %bitcast.334, bf16[]{:T(256)} %broadcast.788), dimensions={1}, to_apply=%bitcast.300.reduce_sub_computation | reduce | bytes 1048578
  88.5 12.4 %all-to-all-done.1 = bf16[16,2,8192]{2,1,0:T(2,128)(2,1)S(1)} async-done(((bf16[16,2,8192]{2,1,0:T(2,128)(2,1)}), bf16[16,2,8192]{2,1,0:T(2,128)(2,1)S(1)}, u32[]{:S(2)}, u32[]{:S(2)}) %all-to-all-start.1) | async-done | bytes 524320 | tf_op jit(solution)/shard_map/all_to_all | solution.py:97
  102.0 12.7 %fusion.8 = f32[128,16,128]{2,0,1:T(8,128)S(1)} fusion(bf16[2048,128,1]{0,1,2:T(8,128)(2,1)S(1)} %reshape.400, f32[2048]{0:T(1024)S(1)} %iota_convert_fusion, f32[16,128]{1,0:T(8,128)S(1)} %bitcast.343), kind=kOutput, calls=%fused_computation.12 | convolution fusion | flops 1128267776 | bytes 1589248 | tf_op jit(solution)/shard_map/dot_general | solution.py:99
  128.5 6.5 %fusion.52 = f32[128,4,16,128]{0,3,2,1:T(8,128)S(1)} fusion(f32[128,4,16,128]{3,2,1,0:T(8,128)S(1)} %get-tuple-element.10), kind=kOutput, calls=%fused_computation.75 | convolution fusion | flops 1610858496 | bytes 8388608 | tf_op jit(solution)/shard_map/...km,mj->...kj/dot_general | solution.py:47
  135.1 6.7 %subtract_bitcast_fusion = f32[128,4,128,16]{0,2,3,1:T(8,128)S(1)} fusion(f32[128,4,16,128]{0,3,2,1:T(8,128)S(1)} %fusion.52, f32[128,4,16,128]{3,2,1,0:T(8,128)S(1)} %get-tuple-element.9), kind=kOutput, calls=%fused_computation.56 | convolution fusion | flops 1611890688 | bytes 12582912 | tf_op jit(solution)/shard_map/...km,mj->...kj/dot_general | solution.py:47
  146.2 9.4 %fusion.50 = f32[128,4,16,128]{0,3,2,1:T(8,128)S(1)} fusion(f32[128,4,16,128]{3,2,1,0:T(8,128)} %copy-done.5), kind=kOutput, calls=%fused_computation.73 | convolution fusion | flops 1610842112 | bytes 8388608 | tf_op jit(solution)/shard_map/...km,mj->...kj/dot_general | solution.py:47
  155.7 6.5 %add_bitcast_fusion = f32[128,4,128,16]{0,2,3,1:T(8,128)S(1)} fusion(f32[128,4,16,128]{0,3,2,1:T(8,128)S(1)} %fusion.50, f32[128,4,16,128]{3,2,1,0:T(8,128)S(1)} %copy-done.4), kind=kOutput, calls=%fused_computation.55 | convolution fusion | flops 1611907072 | bytes 12582912 | tf_op jit(solution)/shard_map/...km,mj->...kj/dot_general | solution.py:47
  166.7 10.4 %reduce-scatter.5.cloned.1.call-done = f32[128,4,1024]{0,2,1:T(8,128)} async-done(((f32[128,4,2048]{0,2,1:T(8,128)}), f32[128,4,1024]{0,2,1:T(8,128)}) %reduce-scatter.5.cloned.1.call-update) | async-done | bytes 2097168 | tf_op jit(solution)/shard_map/reduce_scatter | solution.py:109
  179.7 4.9 copy.123
  184.6 7.0 %all-to-all-start.2 = ((f32[2,128,4,1024]{1,2,0,3:T(4,128)}), f32[2,128,4,1024]{1,2,0,3:T(4,128)}, u32[]{:S(2)}, u32[]{:S(2)}) async-start(f32[2,128,4,1024]{1,2,0,3:T(4,128)} %copy.123), calls=%async_computation.4 | async-start | bytes 8388608 | tf_op jit(solution)/shard_map/all_to_all | solution.py:111
  193.2 78.7 %all-to-all-done.2 = f32[2,128,4,1024]{1,2,0,3:T(4,128)} async-done(((f32[2,128,4,1024]{1,2,0,3:T(4,128)}), f32[2,128,4,1024]{1,2,0,3:T(4,128)}, u32[]{:S(2)}, u32[]{:S(2)}) %all-to-all-start.2) | async-done | bytes 4194336 | tf_op jit(solution)/shard_map/all_to_all | solution.py:111
  298.5 5.6 add_bitcast_fusion.1
  304.1 4.5 copy.127
  308.6 8.7 %fusion.34 = (f32[4,64,16,128]{1,3,2,0:T(8,128)}, f32[4,64,16,128]{1,3,2,0:T(8,128)}) fusion(f32[64,16,128]{0,2,1:T(8,128)S(1)} %copy-done.15, f32[64,16,128]{0,2,1:T(8,128)S(1)} %get-tuple-element.15, f32[4,64,16,128]{1,3,2,0:T(8,128)} %bitcast.325, f32[4,64,16,128]{1,3,2,0:T(8,128)} %bitcast.323), kind=kLoop, calls=%fused_computation.45 | loop fusion | flops 3145728 | bytes 9437184 | tf_op jit(solution)/shard_map/sub | solution.py:126
  349.9 5.6 multiply_bitcast_fusion.2
  364.1 15.3 %copy.181 = f32[2,2048,4,64]{3,2,0,1:T(4,128)} copy(f32[2,2048,4,64]{3,1,2,0:T(8,128)S(1)} %maximum_bitcast_fusion) | data formatting | bytes 8388608 | tf_op jit(solution)/shard_map/transpose | solution.py:129
  379.4 14.6 %reshape.420 = f32[16,1,65536]{2,1,0:T(1,128)} reshape(f32[2048,2,4,64]{3,2,1,0:T(4,128)} %bitcast.312) | data formatting | bytes 8388608
  393.9 113.6 %all_to_all.81 = f32[16,1,65536]{2,1,0:T(1,128)} all-to-all(f32[16,1,65536]{2,1,0:T(1,128)} %reshape.420), channel_id=1, replica_groups=mesh['trans'=16,'los'=2] {'trans'}, dimensions={0} | all-to-all | bytes 8388608 | tf_op jit(solution)/shard_map/all_to_all | solution.py:131
  508.2 13.8 %reduce.2 = f32[16,65536]{1,0:T(8,128)} reduce(f32[16,1,65536]{2,1,0:T(1,128)} %all_to_all.81, f32[]{:T(128)} %broadcast.790), dimensions={1}, to_apply=%all_to_all.69.reduce_sub_computation | reduce | bytes 8388612 | tf_op jit(solution)/shard_map/all_to_all | solution.py:131
  522.0 9.3 %reshape.421 = f32[2048,2,4,64]{3,2,1,0:T(4,128)} reshape(f32[16,65536]{1,0:T(8,128)} %reduce.2) | data formatting | bytes 8388608
  531.2 8.5 %copy.159 = f32[2,16,128,4,64]{2,4,1,3,0:T(8,128)} copy(f32[2,16,128,4,64]{4,3,0,2,1:T(4,128)} %bitcast.311) | data formatting | bytes 8388608 | tf_op jit(solution)/shard_map/all_to_all | solution.py:131
  539.7 5.5 copy.137
  545.3 8.6 %all_to_all.82 = f32[2,128,4,1024]{3,2,0,1:T(4,128)S(1)} all-to-all(f32[2,128,4,1024]{3,2,0,1:T(4,128)} %copy.137), channel_id=1, replica_groups=mesh['trans'=16,'los'=2] {'los'}, dimensions={1} | all-to-all | bytes 8388608 | tf_op jit(solution)/shard_map/all_to_all | solution.py:130
  591.7 4.8 copy.141
  596.5 5.6 multiply_bitcast_fusion
  602.1 4.8 copy.142
  606.9 7.2 %maximum_bitcast_fusion.1 = f32[2,4,64,2048]{2,3,1,0:T(8,128)} fusion(f32[1,64,4,2048]{1,3,2,0:T(8,128)} %bitcast.328, f32[1,64,4,2048]{1,3,2,0:T(8,128)} %bitcast.324), kind=kLoop, calls=%fused_computation.11 | loop fusion | flops 1048576 | bytes 8388608 | tf_op jit(solution)/shard_map/transpose | solution.py:138
  614.1 6.8 %copy.143 = f32[2,4,64,2048]{3,2,1,0:T(8,128)} copy(f32[2,4,64,2048]{2,3,1,0:T(8,128)} %maximum_bitcast_fusion.1) | data formatting | bytes 8388608 | tf_op jit(solution)/shard_map/transpose | solution.py:138
  (125 shorter events, 161.8 us)
Async XLA Ops:
  8.9 21.8 %copy-start.19 = (s32[2]{0:T(128)S(1)}, s32[2]{0:T(128)}, u32[]{:S(2)}) copy-start(s32[2]{0:T(128)} %param.9) | copy-start | bytes 28
  8.9 23.1 %copy-start.16 = (f32[2,2048]{1,0:T(2,128)S(1)}, f32[2,2048]{1,0:T(2,128)}, u32[]{:S(2)}) copy-start(f32[2,2048]{1,0:T(2,128)} %param.8) | copy-start | bytes 49156
  8.9 23.1 %copy-start.17 = (f32[2,2048]{1,0:T(2,128)S(1)}, f32[2,2048]{1,0:T(2,128)}, u32[]{:S(2)}) copy-start(f32[2,2048]{1,0:T(2,128)} %param.7) | copy-start | bytes 49156
  21.8 23.9 %all-to-all-start = ((bf16[16,2,8192]{2,1,0:T(2,128)(2,1)}), bf16[16,2,8192]{2,1,0:T(2,128)(2,1)S(1)}, u32[]{:S(2)}, u32[]{:S(2)}) async-start(bf16[16,2,8192]{2,1,0:T(2,128)(2,1)} %reshape.416), calls=%async_computation | async-start | bytes 1048576 | tf_op jit(solution)/shard_map/all_to_all | solution.py:73
  69.9 16.6 %copy-start.20 = (s32[2]{0:T(128)S(1)}, s32[2]{0:T(128)}, u32[]{:S(2)}) copy-start(s32[2]{0:T(128)} %param.10) | copy-start | bytes 28
  69.9 17.9 %copy-start.18 = (f32[4,2]{0,1:T(2,128)S(1)}, f32[4,2]{0,1:T(2,128)}, u32[]{:S(2)}) copy-start(f32[4,2]{0,1:T(2,128)} %param.11) | copy-start | bytes 100
  82.4 18.4 %all-to-all-start.1 = ((bf16[16,2,8192]{2,1,0:T(2,128)(2,1)}), bf16[16,2,8192]{2,1,0:T(2,128)(2,1)S(1)}, u32[]{:S(2)}, u32[]{:S(2)}) async-start(bf16[16,2,8192]{2,1,0:T(2,128)(2,1)} %reshape.418), calls=%async_computation.1 | async-start | bytes 1048576 | tf_op jit(solution)/shard_map/all_to_all | solution.py:97
  86.4 80.3 %reduce-scatter.3.cloned.1.call-start = ((), (), s32[]{:S(2)}) async-start(), calls=%async_computation.7 | async-start | bytes 6291456 | tf_op jit(solution)/shard_map/reduce_scatter | solution.py:108
  128.5 6.5 %copy-start.5 = (f32[128,4,16,128]{3,2,1,0:T(8,128)}, f32[128,4,16,128]{3,2,1,0:T(8,128)S(1)}, u32[]{:S(2)}) copy-start(f32[128,4,16,128]{3,2,1,0:T(8,128)S(1)} %get-tuple-element.10) | copy-start | bytes 12582916
  128.5 6.5 %copy-start.3 = (f32[128,4,16,128]{3,2,1,0:T(8,128)}, f32[128,4,16,128]{3,2,1,0:T(8,128)S(1)}, u32[]{:S(2)}) copy-start(f32[128,4,16,128]{3,2,1,0:T(8,128)S(1)} %get-tuple-element.9) | copy-start | bytes 12582916
  146.2 31.0 %reduce-scatter.5.cloned.1.call-start = ((), (), s32[]{:S(2)}) async-start(), calls=%async_computation.8 | async-start | bytes 6291456 | tf_op jit(solution)/shard_map/reduce_scatter | solution.py:109
  146.2 9.5 %copy-start.4 = (f32[128,4,16,128]{3,2,1,0:T(8,128)S(1)}, f32[128,4,16,128]{3,2,1,0:T(8,128)}, u32[]{:S(2)}) copy-start(f32[128,4,16,128]{3,2,1,0:T(8,128)} %copy-done.3) | copy-start | bytes 12582916
  184.6 87.3 %all-to-all-start.2 = ((f32[2,128,4,1024]{1,2,0,3:T(4,128)}), f32[2,128,4,1024]{1,2,0,3:T(4,128)}, u32[]{:S(2)}, u32[]{:S(2)}) async-start(f32[2,128,4,1024]{1,2,0,3:T(4,128)} %copy.123), calls=%async_computation.4 | async-start | bytes 8388608 | tf_op jit(solution)/shard_map/all_to_all | solution.py:111
  284.6 6.0 copy-start.1
  304.1 4.5 copy-start.15
  320.4 3.3 copy-start.6
  327.0 1.3 copy-start.8
  328.3 2.0 copy-start.13
  330.2 3.7 copy-start.7
  336.0 5.6 copy-start.2
  564.0 3.3 copy-start.9
  564.0 3.3 copy-start.14
  573.4 1.3 copy-start.11
  574.7 2.0 copy-start.12
  576.7 3.7 copy-start.10
  582.4 5.6 copy-start
Sparse Core Ops, SparseCore 0:
  146.3 10.2 reduce-scatter.2
  166.8 10.2 reduce-scatter.4
where the time goes:
time: 634 us; the launch traced here: 628 us
  local copies, waits for them, and re-layouts  147 us (23%)
  matrix products  145 us (23%)
  blocking collectives  122 us (19%)
  waiting for transfers between devices  115 us (18%)
  other arithmetic  64.5 us (10%)
  starting transfers between devices  19.9 us (3%)
  between operations  14.4 us (2%)
    all_to_all x1, blocking collectives, body(): lax.all_to_all(returned, 'trans', split_axis=1, concat_axis=3, tiled=True)  114 us
    all_to_all x1, waiting for transfers between devices, body(): lax.all_to_all(jnp.stack([summed_real, summed_imag]), 'trans', split_axis...  78.7 us
    dot_general x16, matrix products, second_pass(): return jnp.einsum('...km,mj->...kj', values, table, precision=highest)  74.2 us
    dot_general x16, matrix products, first_pass(): return jnp.einsum('kn,...nm->...km', table, values, precision=highest)  42.8 us
    unnamed x54, local copies, waits for them, and re-layouts  33.2 us
    unnamed x2, other arithmetic  23.1 us
    mul x4, local copies, waits for them, and re-layouts, fourier(): return (out_real * scale, out_imag * scale)  18.3 us
    transpose x1, local copies, waits for them, and re-layouts, body(): returned = jnp.stack([back_real, back_imag]).transpose(0, 3, 1, 2)  15.3 us
  transfers between devices with their start and end apart: 5, of which 4 were waited for; matrix products, arithmetic and copies ran while one was open for 4% of the time, Pallas kernels for 0%

commit v1 on v0

--- a/solution.py
+++ b/solution.py
@@ -127,12 +127,17 @@
     kernel_imag = first_factor * freq_imag + second_factor * freq_real
     back_real, back_imag = fourier(kernel_real, kernel_imag, True)
     returned = jnp.stack([back_real, back_imag]).transpose(0, 3, 1, 2)
+    divide_the_values = lambda patch, lane_axis: jnp.concatenate(
+        jax.lax.all_to_all(
+            jnp.stack(jnp.split(patch, jax.lax.axis_size(lane_axis), 1), axis=0),
+            concat_axis=0,
+            axis_name=lane_axis,
+            split_axis=0,
+        ),
+        axis=3,
+    )
     rows_local = lax.all_to_all(
-        lax.all_to_all(returned, "trans", split_axis=1, concat_axis=3, tiled=True),
-        "los",
-        split_axis=1,
-        concat_axis=3,
-        tiled=True,
+        divide_the_values(returned, "trans"), "los", split_axis=1, concat_axis=3, tiled=True
     )
     final_real, final_imag = fourier(rows_local[0], rows_local[1], True)
     return jnp.stack([final_real, final_imag]).transpose(0, 2, 1, 3)

time: 634 us -> 594 us (0.937)
  local copies, waits for them, and re-layouts: 147 us -> 121 us
  other arithmetic: 64.5 us -> 51 us
    transpose x1 -> x0, local copies, waits for them, and re-layouts: 15.3 us -> none  [body(): returned = jnp.stack([back_real, back_imag]).transpose(0, 3, 1, 2)]
    unnamed x54 -> x63, local copies, waits for them, and re-layouts: 33.2 us -> 19.3 us
    all_to_all x1 -> x0, other arithmetic: 13.8 us -> none  [body(): lax.all_to_all(returned, 'trans', split_axis=1, concat_axis=3, tiled=True)]
    all_to_all x4 -> x2, local copies, waits for them, and re-layouts: 17.1 us -> 4.75 us  [the longest x1 2.43 us: body(): lax.all_to_all(divide_the_values(returned, 'trans'), 'los', split_axis=1,...]
    another operation x0 -> x2, local copies, waits for them, and re-layouts: none -> 7.63 us  [body(): jnp.stack(jnp.split(patch, jax.lax.axis_size(lane_axis), 1), axis=0)]
where the time goes in v1:
time: 594 us; the launch traced here: 588 us
  matrix products  145 us (24%)
  blocking collectives  122 us (21%)
  local copies, waits for them, and re-layouts  121 us (20%)
  waiting for transfers between devices  115 us (19%)
  other arithmetic  51 us (9%)
  starting transfers between devices  19.5 us (3%)
  between operations  14.4 us (2%)
    all_to_all x1, blocking collectives, body(): jax.lax.all_to_all(jnp.stack(jnp.split(patch, jax.lax.axis_size(lane_axis...  114 us
    all_to_all x1, waiting for transfers between devices, body(): lax.all_to_all(jnp.stack([summed_real, summed_imag]), 'trans', split_axis...  78.7 us
    dot_general x16, matrix products, second_pass(): return jnp.einsum('...km,mj->...kj', values, table, precision=highest)  74 us
    dot_general x16, matrix products, first_pass(): return jnp.einsum('kn,...nm->...km', table, values, precision=highest)  43.1 us
    unnamed x2, other arithmetic  23.4 us
    unnamed x63, local copies, waits for them, and re-layouts  19.3 us
    mul x4, local copies, waits for them, and re-layouts, fourier(): return (out_real * scale, out_imag * scale)  18.4 us
    dot_general x4, matrix products, body(): lax.dot_general(by_columns[local_slot], row_block, (((0,), (1,)), ((), ()...  15 us
  transfers between devices with their start and end apart: 5, of which 4 were waited for; matrix products, arithmetic and copies ran while one was open for 4% of the time, Pallas kernels for 0%

profile of v1, /device:TPU:0, one launch (start us, length us, event | category | flops | bytes accessed | tf_op | source)
XLA Modules:
  0.0 588.3 jit_solution(5901417749141465328)
XLA Ops:
  9.5 11.5 %reduce = bf16[2048,128]{1,0:T(8,128)(2,1)S(1)} reduce(bf16[2048,1,128]{2,1,0:T(2,128)(2,1)S(1)} %bitcast.389, bf16[]{:T(256)} %broadcast.788), dimensions={1}, to_apply=%bitcast.336.reduce_sub_computation | reduce | bytes 1048578
  21.9 8.5 %all-to-all-start = ((bf16[16,2,8192]{2,1,0:T(2,128)(2,1)}), bf16[16,2,8192]{2,1,0:T(2,128)(2,1)S(1)}, u32[]{:S(2)}, u32[]{:S(2)}) async-start(bf16[16,2,8192]{2,1,0:T(2,128)(2,1)} %reshape.424), calls=%async_computation | async-start | bytes 1048576 | tf_op jit(solution)/shard_map/all_to_all | solution.py:73
  31.8 13.7 %all-to-all-done = bf16[16,2,8192]{2,1,0:T(2,128)(2,1)S(1)} async-done(((bf16[16,2,8192]{2,1,0:T(2,128)(2,1)}), bf16[16,2,8192]{2,1,0:T(2,128)(2,1)S(1)}, u32[]{:S(2)}, u32[]{:S(2)}) %all-to-all-start) | async-done | bytes 524320 | tf_op jit(solution)/shard_map/all_to_all | solution.py:73
  61.5 8.1 %copy.178 = bf16[1,128,2048]{1,0,2:T(2,128)(2,1)S(1)} copy(bf16[1,128,2048]{1,2,0:T(8,128)(2,1)S(1)} %pad_maximum_fusion.1) | data formatting | bytes 1048576 | tf_op jit(solution)/shard_map/concatenate | solution.py:94
  69.6 11.9 %reduce.1 = bf16[2048,128]{1,0:T(8,128)(2,1)S(1)} reduce(bf16[2048,1,128]{2,1,0:T(2,128)(2,1)S(1)} %bitcast.390, bf16[]{:T(256)} %broadcast.788), dimensions={1}, to_apply=%bitcast.358.reduce_sub_computation | reduce | bytes 1048578
  88.5 12.3 %all-to-all-done.1 = bf16[16,2,8192]{2,1,0:T(2,128)(2,1)S(1)} async-done(((bf16[16,2,8192]{2,1,0:T(2,128)(2,1)}), bf16[16,2,8192]{2,1,0:T(2,128)(2,1)S(1)}, u32[]{:S(2)}, u32[]{:S(2)}) %all-to-all-start.1) | async-done | bytes 524320 | tf_op jit(solution)/shard_map/all_to_all | solution.py:97
  102.0 12.5 %fusion.8 = f32[128,16,128]{2,0,1:T(8,128)S(1)} fusion(bf16[2048,128,1]{0,1,2:T(8,128)(2,1)S(1)} %reshape.408, f32[2048]{0:T(1024)S(1)} %iota_convert_fusion, f32[16,128]{1,0:T(8,128)S(1)} %bitcast.399), kind=kOutput, calls=%fused_computation.12 | convolution fusion | flops 1128267776 | bytes 1589248 | tf_op jit(solution)/shard_map/dot_general | solution.py:99
  128.4 6.5 %fusion.52 = f32[128,4,16,128]{0,3,2,1:T(8,128)S(1)} fusion(f32[128,4,16,128]{3,2,1,0:T(8,128)S(1)} %get-tuple-element.10), kind=kOutput, calls=%fused_computation.75 | convolution fusion | flops 1610858496 | bytes 8388608 | tf_op jit(solution)/shard_map/...km,mj->...kj/dot_general | solution.py:47
  134.9 6.9 %subtract_bitcast_fusion = f32[128,4,128,16]{0,2,3,1:T(8,128)S(1)} fusion(f32[128,4,16,128]{0,3,2,1:T(8,128)S(1)} %fusion.52, f32[128,4,16,128]{3,2,1,0:T(8,128)S(1)} %get-tuple-element.9), kind=kOutput, calls=%fused_computation.56 | convolution fusion | flops 1611890688 | bytes 12582912 | tf_op jit(solution)/shard_map/...km,mj->...kj/dot_general | solution.py:47
  146.3 9.2 %fusion.50 = f32[128,4,16,128]{0,3,2,1:T(8,128)S(1)} fusion(f32[128,4,16,128]{3,2,1,0:T(8,128)} %copy-done.5), kind=kOutput, calls=%fused_computation.73 | convolution fusion | flops 1610842112 | bytes 8388608 | tf_op jit(solution)/shard_map/...km,mj->...kj/dot_general | solution.py:47
  155.5 6.5 %add_bitcast_fusion = f32[128,4,128,16]{0,2,3,1:T(8,128)S(1)} fusion(f32[128,4,16,128]{0,3,2,1:T(8,128)S(1)} %fusion.50, f32[128,4,16,128]{3,2,1,0:T(8,128)S(1)} %copy-done.4), kind=kOutput, calls=%fused_computation.55 | convolution fusion | flops 1611907072 | bytes 12582912 | tf_op jit(solution)/shard_map/...km,mj->...kj/dot_general | solution.py:47
  162.0 4.4 copy.123
  166.5 10.4 %reduce-scatter.5.cloned.1.call-done = f32[128,4,1024]{0,2,1:T(8,128)} async-done(((f32[128,4,2048]{0,2,1:T(8,128)}), f32[128,4,1024]{0,2,1:T(8,128)}) %reduce-scatter.5.cloned.1.call-update) | async-done | bytes 2097168 | tf_op jit(solution)/shard_map/reduce_scatter | solution.py:109
  179.5 5.1 copy.124
  184.6 7.0 %all-to-all-start.2 = ((f32[2,128,4,1024]{1,2,0,3:T(4,128)}), f32[2,128,4,1024]{1,2,0,3:T(4,128)}, u32[]{:S(2)}, u32[]{:S(2)}) async-start(f32[2,128,4,1024]{1,2,0,3:T(4,128)} %copy.124), calls=%async_computation.4 | async-start | bytes 8388608 | tf_op jit(solution)/shard_map/all_to_all | solution.py:111
  193.2 78.7 %all-to-all-done.2 = f32[2,128,4,1024]{1,2,0,3:T(4,128)} async-done(((f32[2,128,4,1024]{1,2,0,3:T(4,128)}), f32[2,128,4,1024]{1,2,0,3:T(4,128)}, u32[]{:S(2)}, u32[]{:S(2)}) %all-to-all-start.2) | async-done | bytes 4194336 | tf_op jit(solution)/shard_map/all_to_all | solution.py:111
  293.9 4.4 copy.128
  298.3 5.6 subtract_bitcast_fusion.1
  303.9 4.5 copy.127
  308.4 8.8 %fusion.34 = (f32[4,64,16,128]{1,3,2,0:T(8,128)}, f32[4,64,16,128]{1,3,2,0:T(8,128)}) fusion(f32[64,16,128]{0,2,1:T(8,128)S(1)} %copy-done.13, f32[64,16,128]{0,2,1:T(8,128)S(1)} %get-tuple-element.15, f32[4,64,16,128]{1,3,2,0:T(8,128)} %bitcast.379, f32[4,64,16,128]{1,3,2,0:T(8,128)} %bitcast.381), kind=kLoop, calls=%fused_computation.45 | loop fusion | flops 3145728 | bytes 9437184 | tf_op jit(solution)/shard_map/sub | solution.py:126
  320.2 4.8 copy.130
  345.8 4.4 copy.134
  350.2 5.6 multiply_bitcast_fusion.3
  377.8 6.8 %copy.135 = f32[16,2,128,4,64]{2,4,3,1,0:T(8,128)} copy(f32[16,2,128,4,64]{4,2,3,1,0:T(8,128)} %fusion.139) | data formatting | bytes 8388608 | tf_op jit(solution)/shard_map/stack | solution.py:132
  384.5 113.5 %all_to_all.68 = f32[16,2,128,4,64]{2,4,3,1,0:T(8,128)S(1)} all-to-all(f32[16,2,128,4,64]{2,4,3,1,0:T(8,128)} %copy.135), channel_id=1, replica_groups=mesh['trans'=16,'los'=2] {'trans'}, dimensions={0} | all-to-all | bytes 8388608 | tf_op jit(solution)/shard_map/all_to_all | solution.py:131
  500.4 5.5 copy.137
  505.9 8.6 %all_to_all.69 = f32[2,128,4,1024]{3,2,0,1:T(4,128)S(1)} all-to-all(f32[2,128,4,1024]{3,2,0,1:T(4,128)} %copy.137), channel_id=1, replica_groups=mesh['trans'=16,'los'=2] {'los'}, dimensions={1} | all-to-all | bytes 8388608 | tf_op jit(solution)/shard_map/all_to_all | solution.py:139
  552.0 4.8 copy.142
  556.8 5.6 multiply_bitcast_fusion.1
  562.4 4.8 copy.141
  567.2 7.2 %maximum_bitcast_fusion.1 = f32[2,4,64,2048]{2,3,1,0:T(8,128)} fusion(f32[1,64,4,2048]{1,3,2,0:T(8,128)} %bitcast.380, f32[1,64,4,2048]{1,3,2,0:T(8,128)} %bitcast.384), kind=kLoop, calls=%fused_computation.11 | loop fusion | flops 1048576 | bytes 8388608 | tf_op jit(solution)/shard_map/transpose | solution.py:143
  574.4 6.8 %copy.143 = f32[2,4,64,2048]{3,2,1,0:T(8,128)} copy(f32[2,4,64,2048]{2,3,1,0:T(8,128)} %maximum_bitcast_fusion.1) | data formatting | bytes 8388608 | tf_op jit(solution)/shard_map/transpose | solution.py:143
  (133 shorter events, 158.8 us)
Async XLA Ops:
  6.5 23.9 %copy-start.17 = (s32[2]{0:T(128)S(1)}, s32[2]{0:T(128)}, u32[]{:S(2)}) copy-start(s32[2]{0:T(128)} %param.9) | copy-start | bytes 28
  6.5 25.1 %copy-start.14 = (f32[2,2048]{1,0:T(2,128)S(1)}, f32[2,2048]{1,0:T(2,128)}, u32[]{:S(2)}) copy-start(f32[2,2048]{1,0:T(2,128)} %param.8) | copy-start | bytes 49156
  6.5 25.1 %copy-start.15 = (f32[2,2048]{1,0:T(2,128)S(1)}, f32[2,2048]{1,0:T(2,128)}, u32[]{:S(2)}) copy-start(f32[2,2048]{1,0:T(2,128)} %param.7) | copy-start | bytes 49156
  21.9 23.6 %all-to-all-start = ((bf16[16,2,8192]{2,1,0:T(2,128)(2,1)}), bf16[16,2,8192]{2,1,0:T(2,128)(2,1)S(1)}, u32[]{:S(2)}, u32[]{:S(2)}) async-start(bf16[16,2,8192]{2,1,0:T(2,128)(2,1)} %reshape.424), calls=%async_computation | async-start | bytes 1048576 | tf_op jit(solution)/shard_map/all_to_all | solution.py:73
  61.4 25.1 %copy-start.18 = (s32[2]{0:T(128)S(1)}, s32[2]{0:T(128)}, u32[]{:S(2)}) copy-start(s32[2]{0:T(128)} %param.10) | copy-start | bytes 28
  61.4 26.3 %copy-start.16 = (f32[4,2]{0,1:T(2,128)S(1)}, f32[4,2]{0,1:T(2,128)}, u32[]{:S(2)}) copy-start(f32[4,2]{0,1:T(2,128)} %param.11) | copy-start | bytes 100
  82.5 18.4 %all-to-all-start.1 = ((bf16[16,2,8192]{2,1,0:T(2,128)(2,1)}), bf16[16,2,8192]{2,1,0:T(2,128)(2,1)S(1)}, u32[]{:S(2)}, u32[]{:S(2)}) async-start(bf16[16,2,8192]{2,1,0:T(2,128)(2,1)} %reshape.426), calls=%async_computation.1 | async-start | bytes 1048576 | tf_op jit(solution)/shard_map/all_to_all | solution.py:97
  86.4 80.1 %reduce-scatter.3.cloned.1.call-start = ((), (), s32[]{:S(2)}) async-start(), calls=%async_computation.7 | async-start | bytes 6291456 | tf_op jit(solution)/shard_map/reduce_scatter | solution.py:108
  128.4 6.5 %copy-start.5 = (f32[128,4,16,128]{3,2,1,0:T(8,128)}, f32[128,4,16,128]{3,2,1,0:T(8,128)S(1)}, u32[]{:S(2)}) copy-start(f32[128,4,16,128]{3,2,1,0:T(8,128)S(1)} %get-tuple-element.10) | copy-start | bytes 12582916
  128.4 6.5 %copy-start.3 = (f32[128,4,16,128]{3,2,1,0:T(8,128)}, f32[128,4,16,128]{3,2,1,0:T(8,128)S(1)}, u32[]{:S(2)}) copy-start(f32[128,4,16,128]{3,2,1,0:T(8,128)S(1)} %get-tuple-element.9) | copy-start | bytes 12582916
  146.2 30.7 %reduce-scatter.5.cloned.1.call-start = ((), (), s32[]{:S(2)}) async-start(), calls=%async_computation.8 | async-start | bytes 6291456 | tf_op jit(solution)/shard_map/reduce_scatter | solution.py:109
  146.3 9.2 %copy-start.4 = (f32[128,4,16,128]{3,2,1,0:T(8,128)S(1)}, f32[128,4,16,128]{3,2,1,0:T(8,128)}, u32[]{:S(2)}) copy-start(f32[128,4,16,128]{3,2,1,0:T(8,128)} %copy-done.3) | copy-start | bytes 12582916
  184.6 87.3 %all-to-all-start.2 = ((f32[2,128,4,1024]{1,2,0,3:T(4,128)}), f32[2,128,4,1024]{1,2,0,3:T(4,128)}, u32[]{:S(2)}, u32[]{:S(2)}) async-start(f32[2,128,4,1024]{1,2,0,3:T(4,128)} %copy.124), calls=%async_computation.4 | async-start | bytes 8388608 | tf_op jit(solution)/shard_map/all_to_all | solution.py:111
  284.6 5.8 copy-start.1
  303.9 4.5 copy-start.13
  320.2 8.3 %copy-start.6 = (f32[4,64,16,128]{3,2,1,0:T(8,128)}, f32[4,64,16,128]{3,2,1,0:T(8,128)S(1)}, u32[]{:S(2)}) copy-start(f32[4,64,16,128]{3,2,1,0:T(8,128)S(1)} %copy.129) | copy-start | bytes 6291460
  330.5 3.7 copy-start.7
  336.3 6.0 %copy-start.2 = (f32[4,64,128,16]{2,3,1,0:T(8,128)}, f32[4,64,128,16]{2,3,1,0:T(8,128)S(1)}, u32[]{:S(2)}) copy-start(f32[4,64,128,16]{2,3,1,0:T(8,128)S(1)} %convolution_subtract_fusion.2) | copy-start | bytes 6291460
  524.6 6.2 %copy-start.8 = (f32[64,4,16,128]{3,2,1,0:T(8,128)}, f32[64,4,16,128]{3,2,1,0:T(8,128)S(1)}, u32[]{:S(2)}) copy-start(f32[64,4,16,128]{3,2,1,0:T(8,128)S(1)} %reshape_squeeze.14) | copy-start | bytes 6291460
  524.6 3.3 copy-start.12
  534.9 3.7 copy-start.10
  534.9 3.7 copy-start.11
  538.7 2.0 copy-start.9
  542.7 5.6 copy-start
Sparse Core Ops, SparseCore 0:
  146.3 10.2 reduce-scatter.2
  166.6 10.2 reduce-scatter.4
